TPU v7x, 16 devices: a whole 2x2x2 slice. The times are simulated.
16 devices in a mesh: rep: 1, dp: 16 (over x, y, z, core).
Axes of the slice: x: 2, y: 2, z: 2, core: 2. Of those that a mesh axis runs over, the one named last changes fastest.
Arguments:
- x: bfloat16 [16, 2048, 896], P(('rep', 'dp'))
- dy: bfloat16 [16, 2048, 896], P(('rep', 'dp'))
- w_gate: bfloat16 [2, 896, 2304], replicated
- w_up: bfloat16 [2, 896, 2304], replicated
- w_down: bfloat16 [2, 2304, 896], replicated
- m_w_gate: float32 [2, 896, 2304], replicated
- m_w_up: float32 [2, 896, 2304], replicated
- m_w_down: float32 [2, 2304, 896], replicated
- v_w_gate: float32 [2, 896, 2304], replicated
- v_w_up: float32 [2, 896, 2304], replicated
- v_w_down: float32 [2, 2304, 896], replicated
Outputs:
- output 1: bfloat16 [2, 896, 2304], P('rep')
- output 2: bfloat16 [2, 896, 2304], P('rep')
- output 3: bfloat16 [2, 2304, 896], P('rep')
- output 4: float32 [2, 896, 2304], P('rep')
- output 5: float32 [2, 896, 2304], P('rep')
- output 6: float32 [2, 2304, 896], P('rep')
- output 7: float32 [2, 896, 2304], P('rep')
- output 8: float32 [2, 896, 2304], P('rep')
- output 9: float32 [2, 2304, 896], P('rep')
All inputs are finite; a program needn't handle non-finite values.
Results may differ from a plain program's by a relative error of at most 0.022.
Values are sent between devices in bfloat16 or wider.
A program may use at most 2.5 GiB of HBM per device.

v0:
```python
import jax
import jax.numpy as jnp
from jax import lax
from jax.sharding import PartitionSpec as P

NAMES = ("w_gate", "w_up", "w_down")


def matmul(a, w):
    return jnp.dot(a, w, preferred_element_type=jnp.float32).astype(jnp.bfloat16)


def normed(h):
    wide = h.astype(jnp.float32)
    scale = lax.rsqrt(jnp.mean(wide**2, -1, keepdims=True) + 1e-6)
    return (wide * scale).astype(jnp.bfloat16)


def layer(h, w):
    a = normed(h)
    gate = jnp.dot(a, w["w_gate"], preferred_element_type=jnp.float32)
    up = jnp.dot(a, w["w_up"], preferred_element_type=jnp.float32)
    return h + matmul((jax.nn.silu(gate) * up).astype(jnp.bfloat16), w["w_down"])


def adamw(w, m, v, g):
    m = 0.9 * m + 0.1 * g
    v = 0.95 * v + 0.05 * g * g
    step = m * lax.rsqrt(v + 1e-8) + 0.1 * w
    return (w - 0.02 * step).astype(jnp.bfloat16), m, v


def clipped(gradients, sum_of_squares, count):
    factor = jnp.minimum(1.0, 0.5 * lax.rsqrt(sum_of_squares / count + 1e-30))
    return [g * factor for g in gradients]


def solution(mesh):
    def step(x, dy, *arrays):
        weights, m, v = (arrays[i : i + 3] for i in (0, 3, 6))
        layers = weights[0].shape[0]
        h, kept = x[0], []
        for number in range(layers):
            kept.append(h)
            h = layer(h, {name: w[number] for name, w in zip(NAMES, weights, strict=True)})
        by_h, summed = dy[0], [None] * layers
        for number in reversed(range(layers)):
            _, back = jax.vjp(lambda w, h: layer(h, w), {name: w[number] for name, w in zip(NAMES, weights, strict=True)}, kept[number])
            by_w, by_h = back(by_h)
            summed[number] = [lax.psum(by_w[name], "dp") for name in NAMES]
        gradients = [jnp.stack([summed[number][i] for number in range(layers)]).astype(jnp.float32) for i in range(3)]
        gradients = clipped(gradients, sum(jnp.sum(g * g) for g in gradients), sum(g.size for g in gradients))
        new = [adamw(w.astype(jnp.float32), m, v, g) for w, m, v, g in zip(weights, m, v, gradients, strict=True)]
        return tuple(one[which] for which in range(3) for one in new)

    return jax.shard_map(
        step,
        mesh=mesh,
        in_specs=(P(("rep", "dp"), None, None),) * 2 + (P(None, None, None),) * 9,
        out_specs=(P("rep", None, None),) * 9,
        check_vma=False,
    )
```

profile of v0, /device:TPU:0, one launch (start us, length us, event | category | flops | bytes accessed | tf_op | source)
XLA Modules:
  0.0 653.2 jit_solution(126371461495814434)
XLA Ops:
  7.2 6.1 copy.20
  16.1 6.1 copy.21
  22.3 15.2 %convolution_convert_fusion.1 = bf16[2048,2304]{1,0:T(8,128)(2,1)} fusion(bf16[2,2304,896]{2,1,0:T(8,128)(2,1)} %param.15, bf16[1,2048,896]{2,1,0:T(8,128)(2,1)} %param.12), kind=kOutput, calls=%fused_computation.63 | convolution fusion | flops 8460435456 | bytes 17235968 | tf_op jit(solution)/shard_map/transpose(jvp())/dot_general | solution.py:10
  37.5 15.5 %fusion.70 = f32[2048,2304]{1,0:T(8,128)} fusion(bf16[2,896,2304]{2,1,0:T(8,128)(2,1)} %param.13, bf16[1,2048,896]{2,1,0:T(8,128)(2,1)S(1)} %copy-done.4, f32[2048]{0:T(1024)S(1)} %add_rsqrt_fusion), kind=kOutput, calls=%fused_computation.105 | convolution fusion | flops 8461221888 | bytes 26681344 | tf_op jit(solution)/shard_map/dot_general | solution.py:21
  53.0 21.6 %multiply_convert_fusion.1 = (bf16[2048,2304]{1,0:T(8,128)(2,1)}, f32[2048,2304]{1,0:T(8,128)}) fusion(f32[2048,2304]{1,0:T(8,128)} %fusion.70, bf16[2,896,2304]{2,1,0:T(8,128)(2,1)} %param.14, bf16[1,2048,896]{2,1,0:T(8,128)(2,1)} %param.11, f32[2048]{0:T(1024)S(1)} %add_rsqrt_fusion), kind=kOutput, calls=%fused_computation.35 | convolution fusion | flops 8489533440 | bytes 54992896 | tf_op jit(solution)/shard_map/dot_general | solution.py:22
  74.6 14.1 %fusion.40 = (f32[2048]{0:T(1024)S(1)}, bf16[2048,896]{0,1:T(8,128)(2,1)S(1)}) fusion(bf16[2048,2304]{1,0:T(8,128)(2,1)} %get-tuple-element.24, bf16[2,2304,896]{2,1,0:T(8,128)(2,1)} %param.15, bf16[1,2048,896]{1,2,0:T(8,128)(2,1)} %copy.20), kind=kOutput, calls=%fused_computation.76 | convolution fusion | flops 8464889856 | bytes 20914176 | tf_op jit(solution)/shard_map/dot_general | solution.py:10
  88.7 16.3 %fusion.57 = f32[2048,2304]{1,0:T(8,128)} fusion(bf16[2,896,2304]{2,1,0:T(8,128)(2,1)} %param.14, bf16[2048,896]{0,1:T(8,128)(2,1)S(1)} %get-tuple-element.27, f32[2048]{0:T(1024)S(1)} %fusion.98), kind=kOutput, calls=%fused_computation.92 | convolution fusion | flops 8461221888 | bytes 26681344 | tf_op jit(solution)/shard_map/jvp()/dot_general | solution.py:22
  105.1 26.4 %fusion.5 = (bf16[2048,2304]{1,0:T(8,128)(2,1)}, f32[2048,2304]{1,0:T(8,128)}) fusion(f32[2048,2304]{1,0:T(8,128)} %fusion.57, bf16[2048,2304]{1,0:T(8,128)(2,1)} %convolution_convert_fusion.1, bf16[2,896,2304]{2,1,0:T(8,128)(2,1)} %param.13, bf16[2048,896]{0,1:T(8,128)(2,1)S(1)} %get-tuple-element.27, f32[2048]{0:T(1024)S(1)} %fusion.98), kind=kOutput, calls=%fused_computation.26 | convolution fusion | flops 8517844992 | bytes 64430080 | tf_op jit(solution)/shard_map/jvp()/dot_general | solution.py:21
  131.4 16.8 %fusion.33 = bf16[2048,896]{0,1:T(8,128)(2,1)} fusion(bf16[2048,2304]{1,0:T(8,128)(2,1)} %convolution_convert_fusion.1, bf16[2,896,2304]{2,1,0:T(8,128)(2,1)} %param.14, f32[2048,2304]{1,0:T(8,128)} %get-tuple-element.29), kind=kOutput, calls=%fused_computation.57 | convolution fusion | flops 8484028416 | bytes 36110336 | tf_op jit(solution)/shard_map/transpose(jvp())/dot_general | solution.py:22
  148.2 18.0 %fusion.53 = bf16[1,896,2304]{2,1,0:T(8,128)(2,1)} fusion(bf16[2048,2304]{1,0:T(8,128)(2,1)} %convolution_convert_fusion.1, bf16[2048,896]{0,1:T(8,128)(2,1)} %copy-done.5, f32[2048]{0:T(1024)S(1)} %fusion.98, f32[2048,2304]{1,0:T(8,128)} %get-tuple-element.29), kind=kOutput, calls=%fused_computation.88 | convolution fusion | flops 8491597824 | bytes 36118528 | tf_op jit(solution)/shard_map/transpose(jvp())/dot_general | solution.py:22
  166.2 19.7 %fusion.55 = bf16[1,2304,896]{2,1,0:T(8,128)(2,1)} fusion(f32[2048,2304]{1,0:T(8,128)} %fusion.57, bf16[1,2048,896]{2,1,0:T(8,128)(2,1)} %param.12, f32[2048,2304]{1,0:T(8,128)} %get-tuple-element.29), kind=kOutput, calls=%fused_computation.90 | convolution fusion | flops 8486092800 | bytes 45547520 | tf_op jit(solution)/shard_map/transpose(jvp())/dot_general | solution.py:10
  185.9 14.6 %fusion.54 = bf16[1,896,2304]{2,1,0:T(8,128)(2,1)} fusion(bf16[2048,2304]{1,0:T(8,128)(2,1)} %get-tuple-element.28, bf16[2048,896]{0,1:T(8,128)(2,1)} %copy-done.5, f32[2048]{0:T(1024)S(1)} %fusion.98), kind=kOutput, calls=%fused_computation.89 | convolution fusion | flops 8461221888 | bytes 17244160 | tf_op jit(solution)/shard_map/transpose(jvp())/dot_general | solution.py:21
  200.5 14.0 %fusion.42 = (f32[2048]{0:T(1024)S(1)}, bf16[2048,896]{0,1:T(8,128)(2,1)S(1)}) fusion(bf16[2048,896]{0,1:T(8,128)(2,1)S(1)} %copy-done.6, bf16[2048,896]{0,1:T(8,128)(2,1)} %fusion.33, bf16[2048,2304]{1,0:T(8,128)(2,1)} %get-tuple-element.28, bf16[2,896,2304]{2,1,0:T(8,128)(2,1)} %param.13), kind=kOutput, calls=%fused_computation.78 | convolution fusion | flops 8464889856 | bytes 24584192 | tf_op jit(solution)/shard_map/transpose(jvp())/dot_general | solution.py:21
  214.5 4.6 fusion.76
  219.2 14.6 %convolution_convert_fusion = bf16[2048,2304]{1,0:T(8,128)(2,1)} fusion(bf16[2048,896]{0,1:T(8,128)(2,1)} %fusion.76, bf16[2,2304,896]{2,1,0:T(8,128)(2,1)S(1)} %bitcast.75), kind=kOutput, calls=%fused_computation.62 | convolution fusion | flops 8460435456 | bytes 17235968 | tf_op jit(solution)/shard_map/transpose(jvp())/dot_general | solution.py:10
  233.8 14.1 %fusion.56 = bf16[1,2304,896]{2,1,0:T(8,128)(2,1)} fusion(bf16[2048,2304]{1,0:T(8,128)(2,1)} %get-tuple-element.24, bf16[2048,896]{0,1:T(8,128)(2,1)S(1)} %copy-done.7), kind=kOutput, calls=%fused_computation.91 | convolution fusion | flops 8457781248 | bytes 17235968 | tf_op jit(solution)/shard_map/transpose(jvp())/dot_general | solution.py:10
  247.9 17.1 %fusion.49 = bf16[1,896,2304]{2,1,0:T(8,128)(2,1)} fusion(bf16[2048,2304]{1,0:T(8,128)(2,1)} %convolution_convert_fusion, bf16[1,2048,896]{1,2,0:T(8,128)(2,1)S(1)} %copy-done.2, f32[2048]{0:T(1024)S(1)} %copy-done.11, f32[2048,2304]{1,0:T(8,128)} %fusion.70), kind=kOutput, calls=%fused_computation.86 | convolution fusion | flops 8491597824 | bytes 36118528 | tf_op jit(solution)/shard_map/transpose(jvp())/dot_general | solution.py:22
  265.0 21.0 %fusion.50 = bf16[1,896,2304]{2,1,0:T(8,128)(2,1)} fusion(f32[2048,2304]{1,0:T(8,128)} %fusion.70, f32[2048,2304]{1,0:T(8,128)} %get-tuple-element.25, bf16[2048,2304]{1,0:T(8,128)(2,1)} %convolution_convert_fusion, bf16[1,2048,896]{1,2,0:T(8,128)(2,1)S(1)} %copy-done.2, f32[2048]{0:T(1024)S(1)} %copy-done.11), kind=kOutput, calls=%fused_computation.87 | convolution fusion | flops 8515190784 | bytes 54992896 | tf_op jit(solution)/shard_map/transpose(jvp())/dot_general | solution.py:21
  286.0 249.7 %all-reduce.3.cloned.1.call-done = (bf16[1,896,2304]{2,1,0:T(8,128)(2,1)}, bf16[1,896,2304]{2,1,0:T(8,128)(2,1)}, bf16[1,896,2304]{2,1,0:T(8,128)(2,1)}, bf16[1,...) async-done(((bf16[1,896,2304]{2,1,0:T(8,128)(2,1)}, bf16[1,896,2304]{2,1,0:T(8,128)(2,1)}, bf16[1,896,2304]{2,1,0:T(8,128)(2,1)}, ...) | async-done | bytes 24772624 | tf_op jit(solution)/shard_map/psum | solution.py:50
  535.7 8.4 %fusion.20 = f32[]{:T(128)} fusion(bf16[1,896,2304]{2,1,0:T(8,128)(2,1)} %get-tuple-element.9, bf16[1,896,2304]{2,1,0:T(8,128)(2,1)} %get-tuple-element.10), kind=kLoop, calls=%fused_computation.44 | loop fusion | flops 16515071 | bytes 8257540 | tf_op jit(solution)/shard_map/reduce_sum | solution.py:52
  544.2 4.8 fusion.21
  550.3 8.3 %fusion.22 = f32[]{:T(128)} fusion(bf16[1,2304,896]{2,1,0:T(8,128)(2,1)} %get-tuple-element.13, bf16[1,2304,896]{2,1,0:T(8,128)(2,1)} %get-tuple-element.14), kind=kLoop, calls=%fused_computation.46 | loop fusion | flops 16515071 | bytes 8257540 | tf_op jit(solution)/shard_map/reduce_sum | solution.py:52
  559.3 28.9 %fusion.28 = (bf16[2,2304,896]{2,1,0:T(8,128)(2,1)}, f32[2,2304,896]{2,1,0:T(8,128)}, f32[2,2304,896]{2,1,0:T(8,128)}) fusion(bf16[2,2304,896]{2,1,0:T(8,128)(2,1)} %param.15, f32[]{:T(128)S(6)} %min_shard_map.3, bf16[1,2304,896]{2,1,0:T(8,128)(2,1)} %get-tuple-element.13, bf16[1,2304,896]{2,1,0:T(8,128)(2,1)} %get-tuple-element.14, ...), kind=kLoop, calls=%fused_computation.52 | loop fusion | flops 82575360 | bytes 90832896 | tf_op jit(solution)/shard_map/convert_element_type | solution.py:30
  588.1 57.8 %fusion.19 = (bf16[2,896,2304]{2,1,0:T(8,128)(2,1)}, f32[2,896,2304]{2,1,0:T(8,128)}, f32[2,896,2304]{2,1,0:T(8,128)}, bf16[2,896,2304]{2,1,0:T(8,128)(2,1)}, f3...) fusion(bf16[2,896,2304]{2,1,0:T(8,128)(2,1)} %param.13, f32[]{:T(128)S(6)} %min_shard_map.3, ...), kind=kLoop, calls=%fused_computation.43 | loop fusion | flops 165150720 | bytes 181665792 | tf_op jit(solution)/shard_map/convert_element_type | solution.py:30
  (35 shorter events, 3.0 us)
Async XLA Ops:
  7.2 528.6 %all-reduce.3.cloned.1.call-start = ((), (), s32[]{:S(2)}) async-start(), calls=%async_computation | async-start | bytes 49545216 | tf_op jit(solution)/shard_map/psum | solution.py:50
  16.1 36.9 %copy-start.10 = (f32[2048]{0:T(1024)}, f32[2048]{0:T(1024)S(1)}, u32[]{:S(2)}) copy-start(f32[2048]{0:T(1024)S(1)} %add_rsqrt_fusion) | copy-start | bytes 24580
  22.3 15.2 %copy-start.4 = (bf16[1,2048,896]{2,1,0:T(8,128)(2,1)S(1)}, bf16[1,2048,896]{2,1,0:T(8,128)(2,1)}, u32[]{:S(2)}) copy-start(bf16[1,2048,896]{2,1,0:T(8,128)(2,1)} %param.11) | copy-start | bytes 11010052
  88.7 16.4 %copy-start.5 = (bf16[2048,896]{0,1:T(8,128)(2,1)}, bf16[2048,896]{0,1:T(8,128)(2,1)S(1)}, u32[]{:S(2)}) copy-start(bf16[2048,896]{0,1:T(8,128)(2,1)S(1)} %get-tuple-element.27) | copy-start | bytes 11010052
  88.7 16.4 %copy-start.8 = (f32[2048]{0:T(1024)}, f32[2048]{0:T(1024)S(1)}, u32[]{:S(2)}) copy-start(f32[2048]{0:T(1024)S(1)} %get-tuple-element.26) | copy-start | bytes 24580
  185.9 14.6 %copy-start.6 = (bf16[2048,896]{0,1:T(8,128)(2,1)S(1)}, bf16[2048,896]{0,1:T(8,128)(2,1)}, u32[]{:S(2)}) copy-start(bf16[2048,896]{0,1:T(8,128)(2,1)} %copy-done.5) | copy-start | bytes 11010052
  185.9 33.2 %slice-start = ((s8[8257536]{0:T(1024)(128)(4,1)}), s8[4194304]{0:T(1024)(128)(4,1)S(1)}, s32[]{:S(2)}) async-start(s8[8257536]{0:T(1024)(128)(4,1)} %bitcast.74), calls=%async_computation.1 | async-start | bytes 8388608
  200.5 14.0 %copy-start.9 = (f32[2048]{0:T(1024)S(1)}, f32[2048]{0:T(1024)}, u32[]{:S(2)}) copy-start(f32[2048]{0:T(1024)} %copy-done.8) | copy-start | bytes 24580
  200.5 14.0 %copy-start.3 = (bf16[1,2048,896]{1,2,0:T(8,128)(2,1)S(1)}, bf16[1,2048,896]{1,2,0:T(8,128)(2,1)}, u32[]{:S(2)}) copy-start(bf16[1,2048,896]{1,2,0:T(8,128)(2,1)} %copy.21) | copy-start | bytes 11010052
  200.5 18.7 %slice-start.1 = ((s8[8257536]{0:T(1024)(128)(4,1)}), s8[4063232]{0:T(1024)(128)(4,1)S(1)}, s32[]{:S(2)}) async-start(s8[8257536]{0:T(1024)(128)(4,1)} %bitcast.74), calls=%async_computation.2 | async-start | bytes 8126464
  219.1 14.6 %copy-start.7 = (bf16[2048,896]{0,1:T(8,128)(2,1)S(1)}, bf16[2048,896]{0,1:T(8,128)(2,1)}, u32[]{:S(2)}) copy-start(bf16[2048,896]{0,1:T(8,128)(2,1)} %fusion.76) | copy-start | bytes 11010052
  233.8 14.1 %copy-start.2 = (bf16[1,2048,896]{1,2,0:T(8,128)(2,1)S(1)}, bf16[1,2048,896]{1,2,0:T(8,128)(2,1)}, u32[]{:S(2)}) copy-start(bf16[1,2048,896]{1,2,0:T(8,128)(2,1)} %copy.20) | copy-start | bytes 11010052
  233.8 14.1 %copy-start.11 = (f32[2048]{0:T(1024)S(1)}, f32[2048]{0:T(1024)}, u32[]{:S(2)}) copy-start(f32[2048]{0:T(1024)} %copy-done.10) | copy-start | bytes 24580
  535.7 8.4 %copy-start = (bf16[1,896,2304]{2,1,0:T(8,128)(2,1)S(1)}, bf16[1,896,2304]{2,1,0:T(8,128)(2,1)}, u32[]{:S(2)}) copy-start(bf16[1,896,2304]{2,1,0:T(8,128)(2,1)} %get-tuple-element.11) | copy-start | bytes 12386308
  535.7 8.4 %copy-start.1 = (bf16[1,896,2304]{2,1,0:T(8,128)(2,1)S(1)}, bf16[1,896,2304]{2,1,0:T(8,128)(2,1)}, u32[]{:S(2)}) copy-start(bf16[1,896,2304]{2,1,0:T(8,128)(2,1)} %get-tuple-element.12) | copy-start | bytes 12386308
Sparse Core Ops, SparseCore 0:
  286.1 249.5 all-reduce.2
where the time goes:
time: 661 us; the launch traced here: 653 us
  matrix products  259 us (39%)
  waiting for transfers between devices  250 us (38%)
  other arithmetic  116 us (18%)
  between operations  16.6 us (3%)
  local copies, waits for them, and re-layouts  12.3 us (2%)
    psum x1, waiting for transfers between devices, step(): summed[number] = [lax.psum(by_w[name], 'dp') for name in NAMES]  250 us
    dot_general x5, matrix products, layer(): gate = jnp.dot(a, w['w_gate'], preferred_element_type=jnp.float32)  91.4 us
    dot_general x5, matrix products, layer(): up = jnp.dot(a, w['w_up'], preferred_element_type=jnp.float32)  89.8 us
    convert_element_type x2, other arithmetic, adamw(): return ((w - 0.02 * step).astype(jnp.bfloat16), m, v)  86.6 us
    dot_general x5, matrix products, matmul(): jnp.dot(a, w, preferred_element_type=jnp.float32).astype(jnp.bfloat16)  77.7 us
    reduce_sum x3, other arithmetic, step(): jnp.sum(g * g)  21.5 us
  transfers between devices with their start and end apart: 1, of which 1 were waited for; matrix products, arithmetic and copies ran while one was open for 0% of the time, Pallas kernels for 0%

commit v1 on v0

v1 whole, which is shorter than its diff:
```python
import functools

import jax
import jax.numpy as jnp
from jax import lax
from jax.experimental import pallas as pl
from jax.experimental.pallas import tpu as pltpu
from jax.sharding import PartitionSpec as P

F32, BF16 = jnp.float32, jnp.bfloat16

LAYERS, T, D, FF = 2, 2048, 896, 2304
NC = 3
FC = FF // NC
RG, RD = D // 8, FC // 16
PANEL = (RG * FC // 2 // 128, 128)
TM = 512
STEPS = T // TM
ORDERS = ((3, 2, 1), (2, 1, 3), (1, 3, 2))
VMEM = 62 * 1024 * 1024


def dot(a, b, ca, cb):
    return lax.dot_general(a, b, (((ca,), (cb,)), ((), ())), preferred_element_type=F32)


def norm_scale(wide):
    return lax.rsqrt(jnp.mean(wide * wide, -1, keepdims=True) + 1e-6)


def normed(h):
    wide = h.astype(F32)
    return (wide * norm_scale(wide)).astype(BF16)


def once(shape, index):
    return pl.BlockSpec(shape, index, pipeline_mode=pl.Buffered(1))


def params(axes=1):
    return pltpu.CompilerParams(dimension_semantics=("arbitrary",) * axes, vmem_limit_bytes=VMEM)


def forward_body(x, wg, wu, wd, a, g, u, h1, a1):
    xv = x[...]
    av = normed(xv)
    a[...] = av
    gv = dot(av, wg[0], 1, 0)
    g[...] = gv
    uv = dot(av, wu[0], 1, 0)
    u[...] = uv
    p = (gv * jax.nn.sigmoid(gv) * uv).astype(BF16)
    hv = (xv.astype(F32) + dot(p, wd[0], 1, 0).astype(BF16).astype(F32)).astype(BF16)
    h1[...] = hv
    a1[...] = normed(hv)


def forward(x, wg, wu, wd):
    row = lambda n: pl.BlockSpec((TM, n), lambda i: (i, 0))
    whole = lambda s: once((1, *s), lambda i: (0, 0, 0))
    return pl.pallas_call(
        forward_body,
        grid=(STEPS,),
        in_specs=[row(D), whole((D, FF)), whole((D, FF)), whole((FF, D))],
        out_specs=[row(D), row(FF), row(FF), row(D), row(D)],
        out_shape=[jax.ShapeDtypeStruct((T, n), t) for n, t in ((D, BF16), (FF, F32), (FF, F32), (D, BF16), (D, BF16))],
        compiler_params=params(),
        cost_estimate=pl.CostEstimate(flops=6 * T * D * FF, bytes_accessed=70_000_000, transcendentals=0),
        name="fwd",
    )(x, wg, wu, wd)


def chunk_body(last_layer, a, dy, *refs):
    if last_layer:
        wg, wu, wd, out, dgo, duo, ag, au, ad = refs
    else:
        gr, ur, wd, out, ag, au, ad = refs
    i = pl.program_id(1)

    @pl.when(i == 0)
    def _():
        ag[...] = jnp.zeros_like(ag)
        au[...] = jnp.zeros_like(au)
        ad[...] = jnp.zeros_like(ad)

    av, dyv = a[...], dy[...]
    if last_layer:
        g = dot(av, wg[0], 1, 0)
        u = dot(av, wu[0], 1, 0)
    else:
        g, u = gr[...], ur[...]
    dp = dot(dyv, wd[0], 1, 1).astype(BF16).astype(F32)
    s = jax.nn.sigmoid(g)
    silu = g * s
    p = (silu * u).astype(BF16)
    du = (dp * silu).astype(BF16)
    dg = (dp * u * (s + silu * (1.0 - s))).astype(BF16)
    if last_layer:
        dgo[...] = dg
        duo[...] = du
    ad[...] += dot(p, dyv, 0, 0)
    ag[...] += dot(av, dg, 0, 0)
    au[...] += dot(av, du, 0, 0)

    @pl.when(i == STEPS - 1)
    def _():
        for c in range(2):
            for k in range(8):

                def put(m, at, value):
                    if last_layer:
                        out[2 * k + c, m, at, :] = value.astype(BF16)
                    else:
                        out[c, m, k, at, :] = value.astype(BF16)

                for m, acc in enumerate((ag, au)):
                    for q in range(3):
                        put(m, slice(q * RG, (q + 1) * RG), acc[k * RG : (k + 1) * RG, c * FC // 2 + q * 128 : c * FC // 2 + (q + 1) * 128])
                row = c * FC // 2 + k * RD
                for q in range(7):
                    put(2, slice(q * RD, (q + 1) * RD), ad[row : row + RD, q * 128 : (q + 1) * 128])


def backward(layer, a, dy, weights, gu=None):
    last = gu is None
    row = lambda n: pl.BlockSpec((TM, n), lambda j, i: (i, 0))
    tile = pl.BlockSpec((TM, FC), lambda j, i: (i, j))
    column = pl.BlockSpec((1, D, FC), lambda j, i: (layer, 0, j))
    rows = pl.BlockSpec((1, FC, D), lambda j, i: (layer, j, 0))
    if last:
        ins, in_specs = weights, [column, column, rows]
        out_specs = [once((16, 3, *PANEL), lambda j, i: (0, j, 0, 0)), tile, tile]
        out_shape = [jax.ShapeDtypeStruct((16, 9, *PANEL), BF16)] + [jax.ShapeDtypeStruct((T, FF), BF16)] * 2
    else:
        ins, in_specs = (*gu, weights[2]), [tile, tile, rows]
        out_specs = once((2, 3, 8, *PANEL), lambda j, i: (0, j, 0, 0, 0))
        out_shape = jax.ShapeDtypeStruct((2, 9, 8, *PANEL), BF16)
    return pl.pallas_call(
        functools.partial(chunk_body, last),
        grid=(NC, STEPS),
        in_specs=[row(D), row(D), *in_specs],
        out_specs=out_specs,
        out_shape=out_shape,
        scratch_shapes=[pltpu.VMEM((D, FC), F32), pltpu.VMEM((D, FC), F32), pltpu.VMEM((FC, D), F32)],
        compiler_params=params(2),
        cost_estimate=pl.CostEstimate(flops=(12 if last else 8) * T * D * FF, bytes_accessed=75_000_000, transcendentals=0),
        name=f"bwd{layer}",
    )(a, dy, *ins)


def input_body(dg, du, wg, wu, h, dy, out):
    by_gate = dot(dg[...], wg[0], 1, 1).astype(BF16).astype(F32)
    by_up = dot(du[...], wu[0], 1, 1).astype(BF16).astype(F32)
    ct = (by_gate + by_up).astype(BF16).astype(F32)
    wide = h[...].astype(F32)
    scale = norm_scale(wide)
    inner = jnp.sum(ct * wide, -1, keepdims=True)
    by_h = ct * scale - wide * (scale * scale * scale * inner * (1.0 / D))
    out[...] = (dy[...].astype(F32) + by_h.astype(BF16).astype(F32)).astype(BF16)


def input_gradient(dg, du, wg, wu, h, dy):
    row = lambda n: pl.BlockSpec((TM, n), lambda i: (i, 0))
    whole = once((1, D, FF), lambda i: (1, 0, 0))
    return pl.pallas_call(
        input_body,
        grid=(STEPS,),
        in_specs=[row(FF), row(FF), whole, whole, row(D), row(D)],
        out_specs=row(D),
        out_shape=jax.ShapeDtypeStruct((T, D), BF16),
        compiler_params=params(),
        cost_estimate=pl.CostEstimate(flops=4 * T * D * FF, bytes_accessed=40_000_000, transcendentals=0),
        name="bwd_in",
    )(dg, du, wg, wu, h, dy)


def reduce_body(g, r1, r0, factor, own, rb0, tot, sb1, rb1, sb2, rb2, sb3, rb3, part, nb, own_sem, core_sem, sem1, sem2, sem3, norm_sem):
    me = lax.axis_index("dp")
    base = {3: me // 8, 2: (me // 4) % 2, 1: (me // 2) % 2}
    core = me % 2
    partner = {b: me + (1 << b) * (1 - 2 * base[b]) for b in (1, 2, 3)}
    partner[0] = me + 1 - 2 * core

    def at(m, t):
        place = {b: 1 - base[b] if (t >> (2 - n)) & 1 else base[b] for n, b in enumerate(ORDERS[m])}
        return 4 * place[3] + 2 * place[2] + place[1]

    def send(src, dst, sems, piece, to):
        return pltpu.make_async_remote_copy(
            src_ref=src, dst_ref=dst, send_sem=sems.at[0, piece], recv_sem=sems.at[1, piece],
            device_id={"dp": to}, device_id_type=pl.DeviceIdType.MESH,
        )

    barrier = pltpu.get_barrier_semaphore()
    for d in range(1, 16):
        pl.semaphore_signal(barrier, inc=1, device_id={"dp": (me + d) % 16}, device_id_type=pl.DeviceIdType.MESH)
    pl.semaphore_wait(barrier, 15)

    def mine(p):
        return pltpu.make_async_copy(g.at[core, p], own.at[p], own_sem.at[p])

    def exchange(p):
        return send(g.at[1 - core, p], rb0.at[p], core_sem, p, partner[0])

    def first(p, m):
        return send(sb1.at[p], rb1.at[p], sem1, p, partner[ORDERS[m][0]])

    def second(p, m):
        return send(sb2.at[p], rb2.at[p], sem2, p, partner[ORDERS[m][1]])

    def third(p, m):
        return send(sb3.at[p], rb3.at[p], sem3, p, partner[ORDERS[m][2]])

    def each(body):
        def at_chunk(j, carry):
            for m in range(3):
                body(3 * j + m, m)
            return carry

        lax.fori_loop(0, NC, at_chunk, 0)

    def start(p, m):
        exchange(p).start()
        mine(p).start()

    each(start)

    def stage1(p, m):
        mine(p).wait()
        exchange(p).wait()
        for t in (4, 5, 6, 7, 0, 1, 2, 3):
            k = at(m, t)
            total = own[p, k].astype(F32) + rb0[p, k].astype(F32)
            if t >= 4:
                sb1[p, t - 4] = total.astype(BF16)
            else:
                tot[p, t] = total
        first(p, m).start()

    def stage2(p, m):
        first(p, m).wait()
        for t in (2, 3, 0, 1):
            total = tot[p, t] + rb1[p, t].astype(F32)
            if t >= 2:
                sb2[p, t - 2] = total.astype(BF16)
            else:
                tot[p, t] = total
        second(p, m).start()

    def stage3(p, m):
        second(p, m).wait()
        sb3[p, 0] = (tot[p, 1] + rb2[p, 1].astype(F32)).astype(BF16)
        tot[p, 0] = tot[p, 0] + rb2[p, 0].astype(F32)
        third(p, m).start()

    each(stage1)
    each(stage2)
    each(stage3)
    part[...] = jnp.zeros_like(part)

    def last(p, m):
        third(p, m).wait()
        r0[p] = (tot[p, 0] + rb3[p, 0].astype(F32)).astype(BF16)
        for r in (r0, r1):
            wide = r[p].astype(F32)
            part[...] += jnp.sum((wide * wide).reshape(PANEL[0] // 8, 8, 128), 0)

    each(last)

    def tell(d):
        return pltpu.make_async_remote_copy(
            src_ref=part, dst_ref=nb.at[me], send_sem=norm_sem.at[0, d], recv_sem=norm_sem.at[1, d],
            device_id={"dp": (me + d) % 16}, device_id_type=pl.DeviceIdType.MESH,
        )

    nb[me] = part[...]
    for d in range(1, 16):
        tell(d).start()
    for d in range(1, 16):
        tell(d).wait()
    total = nb[0]
    for d in range(1, 16):
        total += nb[d]
    squares = jnp.sum(jnp.sum(total, 0, keepdims=True), 1, keepdims=True)
    factor[...] = jnp.broadcast_to(jnp.minimum(1.0, 0.5 * lax.rsqrt(squares / (LAYERS * 3 * D * FF) + 1e-30)), factor.shape)


def reduce(g, r1):
    vmem = pl.BlockSpec(memory_space=pltpu.VMEM)
    buf = lambda n, t=BF16: pltpu.VMEM((9, n, *PANEL), t)
    dma = lambda *n: pltpu.SemaphoreType.DMA(n)
    return pl.pallas_call(
        reduce_body,
        in_specs=[pl.BlockSpec(memory_space=pl.ANY), vmem],
        out_specs=[vmem, vmem],
        out_shape=[jax.ShapeDtypeStruct((9, *PANEL), BF16), jax.ShapeDtypeStruct((8, 128), F32)],
        scratch_shapes=[
            buf(8), buf(8), buf(4, F32), buf(4), buf(4), buf(2), buf(2), buf(1), buf(1),
            pltpu.VMEM((8, 128), F32), pltpu.VMEM((16, 8, 128), F32),
            dma(9), dma(2, 9), dma(2, 9), dma(2, 9), dma(2, 9), dma(2, 16),
        ],
        compiler_params=pltpu.CompilerParams(collective_id=0, has_side_effects=True, vmem_limit_bytes=VMEM),
        cost_estimate=pl.CostEstimate(flops=30_000_000_000, bytes_accessed=20_000_000, transcendentals=0),
        name="reduce0",
    )(g, r1)


def adamw(w, m, v, g):
    m = 0.9 * m + 0.1 * g
    v = 0.95 * v + 0.05 * g * g
    step = m * lax.rsqrt(v + 1e-8) + 0.1 * w
    return (w - 0.02 * step).astype(BF16), m, v


def optimizer_body(factor, g, *refs):
    ins, outs = refs[:9], refs[-9:]
    f = factor[0:1, 0:1]
    for k in range(4):
        for m in range(3):
            w, mo, vo = (ins[n * 3 + m] for n in range(3))
            high = RG if m < 2 else RD
            rows = slice(k * high, (k + 1) * high)
            for q in range(PANEL[0] // high):
                cols = slice(q * 128, (q + 1) * 128)
                gq = g[k, 0, m, q * high : (q + 1) * high, :].astype(F32) * f
                new = adamw(w[0, rows, cols].astype(F32), mo[0, rows, cols], vo[0, rows, cols], gq)
                for n in range(3):
                    outs[n * 3 + m][0, rows, cols] = new[n]


def optimizer(layer, factor, gathered, state, so_far):
    column = pl.BlockSpec((1, D // 2, FC // 2), lambda j, c, r: (layer, r, 2 * j + c))
    rows = pl.BlockSpec((1, FC // 4, D), lambda j, c, r: (layer, 4 * j + 2 * c + r, 0))
    nine = [column, column, rows] * 3
    g = pl.BlockSpec((4, 1, 3, *PANEL), lambda j, c, r: (r, c, j, 0, 0))
    extra = [] if so_far is None else list(so_far)
    return pl.pallas_call(
        optimizer_body,
        grid=(NC, 2, 2),
        in_specs=[once((8, 128), lambda j, c, r: (0, 0)), g, *nine, *([pl.BlockSpec(memory_space=pl.ANY)] * len(extra))],
        out_specs=nine,
        out_shape=[jax.ShapeDtypeStruct(s.shape, s.dtype) for s in state],
        input_output_aliases={11 + n: n for n in range(len(extra))},
        compiler_params=params(3),
        cost_estimate=pl.CostEstimate(flops=15_000_000_000, bytes_accessed=137_000_000, transcendentals=0),
        name=f"adamw{layer}",
    )(factor, gathered.reshape(8, 2, 9, *PANEL), *state, *extra)


def solution(mesh):
    def step(x, dy, *state):
        x, dy = x[0], dy[0]
        weights = state[:3]
        a0, g0, u0, h1, a1 = forward(x, *weights)
        by_w1, dg, du = backward(1, a1, dy, weights)
        summed1 = lax.psum_scatter(by_w1, "dp", scatter_dimension=0)
        by_h = input_gradient(dg, du, weights[0], weights[1], h1, dy)
        by_w0 = backward(0, a0, by_h, weights, (g0, u0))
        summed1, by_w0 = lax.optimization_barrier((summed1, by_w0))
        all1 = lax.all_gather(summed1, "dp")
        summed0, factor = reduce(by_w0, summed1)
        all0 = lax.all_gather(summed0, "dp")
        new = optimizer(1, factor, all1, state, None)
        new = optimizer(0, factor, all0, state, new)
        return tuple(new)

    return jax.shard_map(
        step,
        mesh=mesh,
        in_specs=(P(("rep", "dp"), None, None),) * 2 + (P(None, None, None),) * 9,
        out_specs=(P("rep", None, None),) * 9,
        check_vma=False,
    )
```

time: 661 us -> 417 us (0.63); the launches traced: 653 us -> 417 us
  Pallas kernels: 0 us -> 364 us
  matrix products: 259 us -> 0 us
  waiting for transfers between devices: 250 us -> 38.6 us
  other arithmetic: 116 us -> 0 us
  local copies, waits for them, and re-layouts: 12.3 us -> 0 us
    pallas_call x0 -> x7, Pallas kernels: none -> 364 us  [the longest x2 126 us: backward(): pl.pallas_call(functools.partial(chunk_body, last), grid=(NC, STEPS), in_...]
    dot_general x15 -> x0, matrix products: 259 us -> none  [the longest x5 91.4 us: layer(): gate = jnp.dot(a, w['w_gate'], preferred_element_type=jnp.float32)]
    psum x1 -> x0, waiting for transfers between devices: 250 us -> none  [step(): summed[number] = [lax.psum(by_w[name], 'dp') for name in NAMES]]
    convert_element_type x2 -> x0, other arithmetic: 86.6 us -> none  [adamw(): return ((w - 0.02 * step).astype(jnp.bfloat16), m, v)]
    all_gather x0 -> x2, waiting for transfers between devices: none -> 28.7 us  [the longest x1 18 us: step(): all0 = lax.all_gather(summed0, 'dp')]
    reduce_sum x4 -> x0, other arithmetic: 24.3 us -> none  [the longest x3 21.5 us: step(): jnp.sum(g * g)]
    unnamed x30 -> x0, local copies, waits for them, and re-layouts: 12.3 us -> none
    reduce_scatter x0 -> x1, waiting for transfers between devices: none -> 9.87 us  [step(): summed1 = lax.psum_scatter(by_w1, 'dp', scatter_dimension=0)]
  transfers between devices with their start and end apart: 1 -> 3, of which waited for: 1 -> 3; matrix products, arithmetic and copies ran while one was open for 0% -> 0% of each run, Pallas kernels for 0% -> 50%
where the time goes in v1:
time: 417 us
  Pallas kernels  364 us (87%)
  waiting for transfers between devices  38.6 us (9%)
  between operations  13.8 us (3%)
    pallas_call x2, Pallas kernels, backward(): pl.pallas_call(functools.partial(chunk_body, last), grid=(NC, STEPS), in_...  126 us
    pallas_call x2, Pallas kernels, optimizer(): pl.pallas_call(optimizer_body, grid=(NC, 2, 2), in_specs=[once((8, 128),...  89.9 us
    pallas_call x1, Pallas kernels, reduce(): pl.pallas_call(reduce_body, in_specs=[pl.BlockSpec(memory_space=pl.ANY),...  79.8 us
    pallas_call x1, Pallas kernels, forward(): pl.pallas_call(forward_body, grid=(STEPS,), in_specs=[row(D), whole((D, F...  38.1 us
    pallas_call x1, Pallas kernels, input_gradient(): pl.pallas_call(input_body, grid=(STEPS,), in_specs=[row(FF), row(FF), who...  29.9 us
    all_gather x1, waiting for transfers between devices, step(): all0 = lax.all_gather(summed0, 'dp')  18 us
    all_gather x1, waiting for transfers between devices, step(): all1 = lax.all_gather(summed1, 'dp')  10.7 us
    reduce_scatter x1, waiting for transfers between devices, step(): summed1 = lax.psum_scatter(by_w1, 'dp', scatter_dimension=0)  9.87 us
  transfers between devices with their start and end apart: 3, of which 3 were waited for; matrix products, arithmetic and copies ran while one was open for 0% of the time, Pallas kernels for 50%

profile of v1, /device:TPU:0, one launch (start us, length us, event | category | flops | bytes accessed | tf_op | source)
XLA Modules:
  0.0 416.8 jit_solution(18083353045945926851)
XLA Ops:
  7.2 0.0 reduce-scatter.2.cloned.1.call-start
  7.2 38.1 %fwd.1 = (bf16[2048,896]{1,0:T(8,128)(2,1)}, f32[2048,2304]{1,0:T(8,128)}, f32[2048,2304]{1,0:T(8,128)}, bf16[2048,896]{1,0:T(8,128)(2,1)}, bf16[2048,896]{1,0:T(8,128)(2,1)}) custom-call(bf16[2048,896]{1,0:T(8,128)(2,1)} %bitcast.9, bf16[2,896,2304]{2,1,0:T(8,128)(2,1)} %refs_0_.5, bf16[2,896,2304]{2,1,0:T(8,128)(2,1)} %refs_1_.5, bf16[2,2304,896]{2,1,0:T(8,128)(2,1)} %refs_2_.7), custom_call_target="tpu_custom_call" | custom-call | flops 25367150592 | bytes 70000000 | tf_op jit(solution)/shard_map/fwd/pallas_call | solution.py:61
  45.3 72.7 %bwd1.1 = (bf16[16,9,336,128]{3,2,1,0:T(8,128)(2,1)}, bf16[2048,2304]{1,0:T(8,128)(2,1)}, bf16[2048,2304]{1,0:T(8,128)(2,1)}) custom-call(bf16[2048,896]{1,0:T(8,128)(2,1)} %get-tuple-element.30.a, bf16[2048,896]{1,0:T(8,128)(2,1)} %bitcast.10, bf16[2,896,2304]{2,1,0:T(8,128)(2,1)} %refs_0_.5, bf16[2,896,2304]{2,1,0:T(8,128)(2,1)} %refs_1_.5, ...), custom_call_target="tpu_custom_call" | custom-call | flops 50734301184 | bytes 75000000 | tf_op jit(solution)/shard_map/bwd1/pallas_call | solution.py:138
  118.0 0.0 reduce-scatter.2.cloned.1.call-update
  118.0 0.2 all-gather.7.cloned.1.call-start
  118.3 29.9 %bwd_in.1.dy = bf16[2048,896]{1,0:T(8,128)(2,1)} custom-call(bf16[2048,2304]{1,0:T(8,128)(2,1)} %get-tuple-element.33.dg, bf16[2048,2304]{1,0:T(8,128)(2,1)} %get-tuple-element.34.du, bf16[2,896,2304]{2,1,0:T(8,128)(2,1)} %refs_0_.5, bf16[2,896,2304]{2,1,0:T(8,128)(2,1)} %refs_1_.5, bf16[2048,896]{1,0:T(8,128)(2,1)} %get-tuple-element.35.h, ...), custom_call_target="tpu_custom_call" | custom-call | flops 16911433728 | bytes 40000000 | tf_op jit(solution)/shard_map/bwd_in/pallas_call | solution.py:165
  148.2 53.5 %bwd0.1.g = bf16[2,9,8,336,128]{4,3,2,1,0:T(8,128)(2,1)} custom-call(bf16[2048,896]{1,0:T(8,128)(2,1)} %get-tuple-element.32.a, bf16[2048,896]{1,0:T(8,128)(2,1)} %bwd_in.1.dy, f32[2048,2304]{1,0:T(8,128)} %get-tuple-element.36.refs_0_, f32[2048,2304]{1,0:T(8,128)} %get-tuple-element.37.refs_1_, bf16[2,2304,896]{2,1,0:T(8,128)(2,1)} %refs_2_.7), custom_call_target="tpu_custom_call" | custom-call | flops 33822867456 | bytes 75000000 | tf_op jit(solution)/shard_map/bwd0/pallas_call | solution.py:138
  201.7 9.9 %reduce-scatter.2.cloned.1.call-done = bf16[1,9,336,128]{3,2,1,0:T(8,128)(2,1)} async-done(((bf16[16,9,336,128]{3,2,1,0:T(8,128)(2,1)}), bf16[1,9,336,128]{3,2,1,0:T(8,128)(2,1)}) %reduce-scatter.2.cloned.1.call-update) | async-done | bytes 774160 | tf_op jit(solution)/shard_map/reduce_scatter | solution.py:356
  211.5 0.0 all-gather.7.cloned.1.call-update
  211.5 0.3 all-gather.5.cloned.1.call-start
  211.8 79.8 %reduce0.1 = (bf16[9,336,128]{2,1,0:T(8,128)(2,1)}, f32[8,128]{1,0:T(8,128)}) custom-call(bf16[2,9,8,336,128]{4,3,2,1,0:T(8,128)(2,1)} %bwd0.1.g, bf16[9,336,128]{2,1,0:T(8,128)(2,1)} %bitcast.8), custom_call_target="tpu_custom_call" | custom-call | flops 30000001024 | bytes 20000000 | tf_op jit(solution)/shard_map/reduce0/pallas_call | solution.py:292
  291.6 0.0 all-gather.5.cloned.1.call-update
  291.6 10.7 %all-gather.7.cloned.1.call-done = bf16[144,336,128]{2,1,0:T(8,128)(2,1)} async-done(((bf16[9,336,128]{2,1,0:T(8,128)(2,1)}), bf16[144,336,128]{2,1,0:T(8,128)(2,1)}) %all-gather.7.cloned.1.call-update) | async-done | bytes 12386320 | tf_op jit(solution)/shard_map/all_gather | solution.py:360
  302.3 45.0 %adamw1.1 = (bf16[2,896,2304]{2,1,0:T(8,128)(2,1)}, bf16[2,896,2304]{2,1,0:T(8,128)(2,1)}, bf16[2,2304,896]{2,1,0:T(8,128)(2,1)}, f32[2,896,2304]{2,1,0:T(8,128)...) custom-call(f32[8,128]{1,0:T(8,128)} %get-tuple-element.40.factor, ...), custom_call_target="tpu_custom_call" | custom-call | flops 15000000512 | bytes 137000000 | tf_op jit(solution)/shard_map/adamw1/pallas_call | solution.py:337
  347.2 18.0 %all-gather.5.cloned.1.call-done = bf16[144,336,128]{2,1,0:T(8,128)(2,1)} async-done(((bf16[9,336,128]{2,1,0:T(8,128)(2,1)}), bf16[144,336,128]{2,1,0:T(8,128)(2,1)}) %all-gather.5.cloned.1.call-update) | async-done | bytes 12386320 | tf_op jit(solution)/shard_map/all_gather | solution.py:362
  365.3 44.9 %adamw0.1 = (bf16[2,896,2304]{2,1,0:T(8,128)(2,1)}, bf16[2,896,2304]{2,1,0:T(8,128)(2,1)}, bf16[2,2304,896]{2,1,0:T(8,128)(2,1)}, f32[2,896,2304]{2,1,0:T(8,128)...) custom-call(f32[8,128]{1,0:T(8,128)} %get-tuple-element.40.factor, ...), custom_call_target="tpu_custom_call", output_to_operand_aliasing={{0}: (11, {}), {1}: (12, {}), {2}: (13, {}), {3}: (14, {}),... | custom-call | flops 15000000512 | bytes 137000000 | tf_op jit(solution)/shard_map/adamw0/pallas_call | solution.py:337
Async XLA Ops:
  7.2 204.3 %reduce-scatter.2.cloned.1.call-start = ((), (), s32[]{:S(2)}) async-start(), calls=%async_computation.1 | async-start | bytes 13160448 | tf_op jit(solution)/shard_map/reduce_scatter | solution.py:356
  118.0 184.2 %all-gather.7.cloned.1.call-start = ((), (), s32[]{:S(2)}) async-start(), calls=%async_computation.3 | async-start | bytes 13160448 | tf_op jit(solution)/shard_map/all_gather | solution.py:360
  211.5 153.7 %all-gather.5.cloned.1.call-start = ((), (), s32[]{:S(2)}) async-start(), calls=%async_computation.2 | async-start | bytes 13160448 | tf_op jit(solution)/shard_map/all_gather | solution.py:362
Sparse Core Ops, SparseCore 0:
  118.2 93.3 reduce-scatter.1
  213.7 88.4 all-gather.6
  304.5 60.7 all-gather.4

commit v2 on v0

v2 whole, which is shorter than its diff:
```python
import functools

import jax
import jax.numpy as jnp
from jax import lax
from jax.experimental import pallas as pl
from jax.experimental.pallas import tpu as pltpu
from jax.sharding import PartitionSpec as P

F32, BF16 = jnp.float32, jnp.bfloat16

LAYERS, T, D, FF = 2, 2048, 896, 2304
FB = 256
NB = FF // FB
SPLIT = {1: 5, 0: 4}
TM = 512
RG = D // 8
PANEL = (RG, 128)
ORDERS = ((3, 2, 1), (2, 1, 3), (1, 3, 2))
MESH_ID = pl.DeviceIdType.MESH
VMEM = 62 * 1024 * 1024


def dot(a, b, ca, cb):
    return lax.dot_general(a, b, (((ca,), (cb,)), ((), ())), preferred_element_type=F32)


def norm_scale(wide):
    return lax.rsqrt(jnp.mean(wide * wide, -1, keepdims=True) + 1e-6)


def normed(h):
    wide = h.astype(F32)
    return (wide * norm_scale(wide)).astype(BF16)


def once(shape, index):
    return pl.BlockSpec(shape, index, pipeline_mode=pl.Buffered(1))


def params(**more):
    return pltpu.CompilerParams(dimension_semantics=("arbitrary",), vmem_limit_bytes=VMEM, **more)


def cost(flops, bytes_accessed):
    return pl.CostEstimate(flops=flops, bytes_accessed=bytes_accessed, transcendentals=0)


ANY = pl.BlockSpec(memory_space=pl.ANY)


def forward_body(x, dy, wg, wu, wd, at0, dyt, g, u, h1, a1, at1):
    xv = x[...]
    av = normed(xv)
    at0[...] = av.T
    dyt[...] = dy[...].T
    gv = dot(av, wg[0], 1, 0)
    g[...] = gv
    uv = dot(av, wu[0], 1, 0)
    u[...] = uv
    p = (gv * jax.nn.sigmoid(gv) * uv).astype(BF16)
    hv = (xv.astype(F32) + dot(p, wd[0], 1, 0).astype(BF16).astype(F32)).astype(BF16)
    h1[...] = hv
    av = normed(hv)
    a1[...] = av
    at1[...] = av.T


def forward(x, dy, wg, wu, wd):
    row = lambda n: pl.BlockSpec((TM, n), lambda i: (i, 0))
    col = pl.BlockSpec((D, TM), lambda i: (0, i))
    whole = lambda s: once((1, *s), lambda i: (0, 0, 0))
    flat = lambda a, b, t=BF16: jax.ShapeDtypeStruct((a, b), t)
    return pl.pallas_call(
        forward_body,
        grid=(T // TM,),
        in_specs=[row(D), row(D), whole((D, FF)), whole((D, FF)), whole((FF, D))],
        out_specs=[col, col, row(FF), row(FF), row(D), row(D), col],
        out_shape=[flat(D, T), flat(D, T), flat(T, FF, F32), flat(T, FF, F32), flat(T, D), flat(T, D), flat(D, T)],
        compiler_params=params(),
        cost_estimate=cost(6 * T * D * FF, 75_000_000),
        name="fwd",
    )(x, dy, wg, wu, wd)


class Reduction:
    def __init__(self, nb, g, scratch):
        self.nb, self.g = nb, g
        self.own, self.rb0, self.tot, self.sb1, self.rb1, self.sb2, self.rb2, self.sb3, self.rb3, self.own_sem, *self.sems = scratch
        self.me = me = lax.axis_index("dp")
        self.base = {3: me // 8, 2: (me // 4) % 2, 1: (me // 2) % 2}
        self.core = me % 2
        self.partner = {b: me + (1 << b) * (1 - 2 * self.base[b]) for b in (1, 2, 3)}
        self.partner[0] = me + 1 - 2 * self.core

    @staticmethod
    def scratch(nb):
        n = 3 * nb
        buf = lambda slabs, t=BF16: pltpu.VMEM((n, slabs, *PANEL), t)
        pair = pltpu.SemaphoreType.DMA((2, n))
        return [buf(8), buf(8), buf(4, F32), buf(4), buf(4), buf(2), buf(2), buf(1), buf(1), pltpu.SemaphoreType.DMA((n,)), pair, pair, pair, pair]

    def at(self, m, t):
        place = {b: 1 - self.base[b] if (t >> (2 - n)) & 1 else self.base[b] for n, b in enumerate(ORDERS[m])}
        return 4 * place[3] + 2 * place[2] + place[1]

    def send(self, stage, src, dst, p, to):
        sems = self.sems[stage]
        return pltpu.make_async_remote_copy(
            src_ref=src, dst_ref=dst, send_sem=sems.at[0, p], recv_sem=sems.at[1, p], device_id={"dp": self.partner[to]}, device_id_type=MESH_ID
        )

    def mine(self, p, m, b):
        return pltpu.make_async_copy(self.g.at[self.core, m, b], self.own.at[p], self.own_sem.at[p])

    def exchange(self, p, m, b):
        return self.send(0, self.g.at[1 - self.core, m, b], self.rb0.at[p], p, 0)

    def first(self, p, m):
        return self.send(1, self.sb1.at[p], self.rb1.at[p], p, ORDERS[m][0])

    def second(self, p, m):
        return self.send(2, self.sb2.at[p], self.rb2.at[p], p, ORDERS[m][1])

    def third(self, p, m):
        return self.send(3, self.sb3.at[p], self.rb3.at[p], p, ORDERS[m][2])

    def each(self, body):
        def at_block(b, carry):
            for m in range(3):
                body(3 * b + m, m, b)
            return carry

        lax.fori_loop(0, self.nb, at_block, 0)

    def barrier(self, everyone=False):
        others = [(self.me + d) % 16 for d in range(1, 16)] if everyone else [self.partner[b] for b in range(4)]
        semaphore = pltpu.get_barrier_semaphore()
        for other in others:
            pl.semaphore_signal(semaphore, inc=1, device_id={"dp": other}, device_id_type=MESH_ID)
        pl.semaphore_wait(semaphore, len(others))

    def start(self):
        def body(p, m, b):
            self.exchange(p, m, b).start()
            self.mine(p, m, b).start()

        self.each(body)

    def stage1(self):
        def body(p, m, b):
            self.mine(p, m, b).wait()
            self.exchange(p, m, b).wait()
            for t in (4, 5, 6, 7, 0, 1, 2, 3):
                k = self.at(m, t)
                total = self.own[p, k].astype(F32) + self.rb0[p, k].astype(F32)
                if t >= 4:
                    self.sb1[p, t - 4] = total.astype(BF16)
                else:
                    self.tot[p, t] = total
            self.first(p, m).start()

        self.each(body)

    def stage2(self):
        def body(p, m, b):
            self.first(p, m).wait()
            for t in (2, 3, 0, 1):
                total = self.tot[p, t] + self.rb1[p, t].astype(F32)
                if t >= 2:
                    self.sb2[p, t - 2] = total.astype(BF16)
                else:
                    self.tot[p, t] = total
            self.second(p, m).start()

        self.each(body)

    def stage3(self):
        def body(p, m, b):
            self.second(p, m).wait()
            self.sb3[p, 0] = (self.tot[p, 1] + self.rb2[p, 1].astype(F32)).astype(BF16)
            self.tot[p, 0] = self.tot[p, 0] + self.rb2[p, 0].astype(F32)
            self.third(p, m).start()

        self.each(body)

    def finish(self, r, at=0):
        def body(p, m, b):
            self.third(p, m).wait()
            r[m, at + b] = (self.tot[p, 0] + self.rb3[p, 0].astype(F32)).astype(BF16)

        self.each(body)

    def hooks(self, b, after, r, at=0):
        def before():
            @pl.when(b == 0)
            def _():
                self.barrier()
                self.start()

        def behind():
            for step in sorted(set(after)):

                @pl.when(b == step)
                def _():
                    for n, stage in enumerate((self.stage1, self.stage2, self.stage3, lambda: self.finish(r, at))):
                        if after[n] == step:
                            stage()

        return before, behind


def block_body(last, hook, *refs):
    refs = list(refs)
    take = lambda n: [refs.pop(0) for _ in range(n)]
    at, dyt, dy = take(3)
    a, wg, wu = take(3) if last else (None, None, None)
    gr, ur = take(2) if not last else (None, None)
    (wd,) = take(1)
    g_before = take(1)[0] if hook else None
    (out,) = take(1)
    dgo, duo = take(2) if last else (None, None)
    r = take(1)[0] if hook else None
    ps, dgs, dus, atv, dytv, sem = take(6)
    b = pl.program_id(0)
    if hook:
        before, behind = Reduction(hook[0], g_before, refs).hooks(b, hook[1], r)
        before()
    loads = pltpu.make_async_copy(at, atv, sem.at[0]), pltpu.make_async_copy(dyt, dytv, sem.at[1])

    @pl.when(b == 0)
    def _():
        for load in loads:
            load.start()

    for i in range(T // TM):
        rows = slice(i * TM, (i + 1) * TM)
        dp = dot(dy[rows, :], wd[0], 1, 1).astype(BF16).astype(F32)
        if last:
            g = dot(a[rows, :], wg[0], 1, 0)
            u = dot(a[rows, :], wu[0], 1, 0)
        else:
            g, u = gr[rows, :], ur[rows, :]
        s = jax.nn.sigmoid(g)
        silu = g * s
        ps[rows, :] = (silu * u).astype(BF16)
        du = (dp * silu).astype(BF16)
        dg = (dp * u * (s + silu * (1.0 - s))).astype(BF16)
        dgs[rows, :] = dg
        dus[rows, :] = du
        if last:
            dgo[rows, :] = dg
            duo[rows, :] = du

    @pl.when(b == 0)
    def _():
        for load in loads:
            load.wait()

    for m, (lhs, rhs) in enumerate(((atv, dgs), (atv, dus), (dytv, ps))):
        full = dot(lhs[...], rhs[...], 1, 0)
        for k in range(8):
            for c in range(2):
                out[c, m, 0, k] = full[k * RG : (k + 1) * RG, c * 128 : (c + 1) * 128].astype(BF16)
    if hook:
        behind()


def backward(layer, begin, n, at, dyt, dy, weights, a=None, gu=None, before=None, after=None):
    last = gu is None
    full = lambda s: once(s, lambda b: (0, 0))
    tile = pl.BlockSpec((T, FB), lambda b: (0, begin + b))
    column = pl.BlockSpec((1, D, FB), lambda b: (layer, 0, begin + b))
    rows = pl.BlockSpec((1, FB, D), lambda b: (layer, begin + b, 0))
    ins, in_specs = ((a, *weights), [full((T, D)), column, column, rows]) if last else ((*gu, weights[2]), [tile, tile, rows])
    out_specs = [pl.BlockSpec((2, 3, 1, 8, *PANEL), lambda b: (0, 0, b, 0, 0, 0))]
    out_shape = [jax.ShapeDtypeStruct((2, 3, n, 8, *PANEL), BF16)]
    if last:
        out_specs += [pl.BlockSpec((T, FB), lambda b: (0, b))] * 2
        out_shape += [jax.ShapeDtypeStruct((T, n * FB), BF16)] * 2
    scratch = [pltpu.VMEM((T, FB), BF16)] * 3 + [pltpu.VMEM((D, T), BF16)] * 2 + [pltpu.SemaphoreType.DMA((2,))]
    hook, more = None, {}
    if before is not None:
        nb = before.shape[2]
        hook, more = (nb, after), dict(collective_id=2 + layer, has_side_effects=True)
        ins, in_specs = (*ins, before), [*in_specs, ANY]
        out_specs.append(once((3, nb, *PANEL), lambda b: (0, 0, 0, 0)))
        out_shape.append(jax.ShapeDtypeStruct((3, nb, *PANEL), BF16))
        scratch += Reduction.scratch(nb)
    return pl.pallas_call(
        functools.partial(block_body, last, hook),
        grid=(n,),
        in_specs=[ANY, ANY, full((T, D)), *in_specs],
        out_specs=out_specs,
        out_shape=out_shape,
        scratch_shapes=scratch,
        compiler_params=params(**more),
        cost_estimate=cost((12 if last else 8) * T * D * FB * n, 8_000_000 * n),
        name=f"bwd{layer}{'ab'[hook is not None]}",
    )(at, dyt, dy, *ins)


def input_body(after, dga, dgb, dua, dub, wg, wu, h, dy, g_before, r_before, out, out_t, r, *scratch):
    b = pl.program_id(0)
    cut = dga.shape[1]
    nb = g_before.shape[2]
    before, behind = Reduction(nb, g_before, scratch).hooks(b, after, r, NB - nb)
    before()

    @pl.when(b == 0)
    def _():
        r[:, : NB - nb] = r_before[...]

    by_gate = dot(dga[...], wg[0, :, :cut], 1, 1) + dot(dgb[...], wg[0, :, cut:], 1, 1)
    by_up = dot(dua[...], wu[0, :, :cut], 1, 1) + dot(dub[...], wu[0, :, cut:], 1, 1)
    ct = (by_gate.astype(BF16).astype(F32) + by_up.astype(BF16).astype(F32)).astype(BF16).astype(F32)
    wide = h[...].astype(F32)
    scale = norm_scale(wide)
    inner = jnp.sum(ct * wide, -1, keepdims=True)
    by_h = ct * scale - wide * (scale * scale * scale * inner * (1.0 / D))
    new = (dy[...].astype(F32) + by_h.astype(BF16).astype(F32)).astype(BF16)
    out[...] = new
    out_t[...] = new.T
    behind()


def input_gradient(dgs, dus, wg, wu, h, dy, g_before, r_before, after):
    tm = 256
    row = lambda n: pl.BlockSpec((tm, n), lambda i: (i, 0))
    whole = once((1, D, FF), lambda i: (1, 0, 0))
    part = lambda n: once((3, n, *PANEL), lambda i: (0, 0, 0, 0))
    nb = g_before.shape[2]
    return pl.pallas_call(
        functools.partial(input_body, after),
        grid=(T // tm,),
        in_specs=[*(row(t.shape[1]) for t in (*dgs, *dus)), whole, whole, row(D), row(D), ANY, part(NB - nb)],
        out_specs=[row(D), pl.BlockSpec((D, tm), lambda i: (0, i)), part(NB)],
        out_shape=[jax.ShapeDtypeStruct(s, BF16) for s in ((T, D), (D, T), (3, NB, *PANEL))],
        scratch_shapes=Reduction.scratch(nb),
        compiler_params=params(collective_id=1, has_side_effects=True),
        cost_estimate=cost(4 * T * D * FF, 40_000_000),
        name="bwd_in",
    )(*dgs, *dus, wg, wu, h, dy, g_before, r_before)


def reduce_body(g, r_before, r1, r0, factor, part, nb, norm_sem, *scratch):
    blocks = g.shape[2]
    reduction = Reduction(blocks, g, scratch)
    me = reduction.me
    reduction.barrier(True)
    reduction.start()
    r0[:, : NB - blocks] = r_before[...]
    reduction.stage1()
    reduction.stage2()
    reduction.stage3()
    reduction.finish(r0, NB - blocks)
    part[...] = jnp.zeros_like(part)

    def squares(b, carry):
        for m in range(3):
            for r in (r0, r1):
                wide = r[m, b].astype(F32)
                part[...] += jnp.sum((wide * wide).reshape(RG // 8, 8, 128), 0)
        return carry

    lax.fori_loop(0, NB, squares, 0)

    def tell(d):
        return pltpu.make_async_remote_copy(
            src_ref=part, dst_ref=nb.at[me], send_sem=norm_sem.at[0, d], recv_sem=norm_sem.at[1, d],
            device_id={"dp": (me + d) % 16}, device_id_type=MESH_ID,
        )

    nb[me] = part[...]
    for d in range(1, 16):
        tell(d).start()
    for d in range(1, 16):
        tell(d).wait()
    total = nb[0]
    for d in range(1, 16):
        total += nb[d]
    total = jnp.sum(jnp.sum(total, 0, keepdims=True), 1, keepdims=True)
    factor[...] = jnp.broadcast_to(jnp.minimum(1.0, 0.5 * lax.rsqrt(total / (LAYERS * 3 * D * FF) + 1e-30)), factor.shape)


def reduce(g, r_before, r1):
    vmem = pl.BlockSpec(memory_space=pltpu.VMEM)
    return pl.pallas_call(
        reduce_body,
        in_specs=[ANY, vmem, vmem],
        out_specs=[vmem, vmem],
        out_shape=[jax.ShapeDtypeStruct((3, NB, *PANEL), BF16), jax.ShapeDtypeStruct((8, 128), F32)],
        scratch_shapes=[pltpu.VMEM((8, 128), F32), pltpu.VMEM((16, 8, 128), F32), pltpu.SemaphoreType.DMA((2, 16)), *Reduction.scratch(g.shape[2])],
        compiler_params=pltpu.CompilerParams(collective_id=0, has_side_effects=True, vmem_limit_bytes=VMEM),
        cost_estimate=cost(20_000_000_000, 20_000_000),
        name="reduce0",
    )(g, r_before, r1)


def adamw(w, m, v, g):
    m = 0.9 * m + 0.1 * g
    v = 0.95 * v + 0.05 * g * g
    step = m * lax.rsqrt(v + 1e-8) + 0.1 * w
    return (w - 0.02 * step).astype(BF16), m, v


def optimizer_body(factor, g, *refs):
    ins, outs = refs[:9], refs[-9:]
    f = factor[0:1, 0:1]
    for m in range(3):
        w, mo, vo = (ins[n * 3 + m] for n in range(3))
        for c in range(2):
            half = slice(c * 128, (c + 1) * 128)
            if m < 2:
                for k in range(8):
                    rows = slice(k * RG, (k + 1) * RG)
                    new = adamw(w[0, rows, half].astype(F32), mo[0, rows, half], vo[0, rows, half], g[k, c, m, 0].astype(F32) * f)
                    for n in range(3):
                        outs[n * 3 + m][0, rows, half] = new[n]
            else:
                turned = jnp.concatenate([g[k, c, m, 0].astype(F32) for k in range(8)], 0).T
                new = adamw(w[0, half, :].astype(F32), mo[0, half, :], vo[0, half, :], turned * f)
                for n in range(3):
                    outs[n * 3 + m][0, half, :] = new[n]


def optimizer(layer, factor, gathered, state, so_far):
    column = pl.BlockSpec((1, D, FB), lambda b: (layer, 0, b))
    rows = pl.BlockSpec((1, FB, D), lambda b: (layer, b, 0))
    nine = [column, column, rows] * 3
    g = pl.BlockSpec((8, 2, 3, 1, *PANEL), lambda b: (0, 0, 0, b, 0, 0))
    extra = [] if so_far is None else list(so_far)
    return pl.pallas_call(
        optimizer_body,
        grid=(NB,),
        in_specs=[once((8, 128), lambda b: (0, 0)), g, *nine, *([ANY] * len(extra))],
        out_specs=nine,
        out_shape=[jax.ShapeDtypeStruct(s.shape, s.dtype) for s in state],
        input_output_aliases={11 + n: n for n in range(len(extra))},
        compiler_params=params(),
        cost_estimate=cost(15_000_000_000, 137_000_000),
        name=f"adamw{layer}",
    )(factor, gathered.reshape(8, 2, 3, NB, *PANEL), *state, *extra)


def gather(part):
    return lax.all_gather(part.reshape(-1, *PANEL), "dp")


def solution(mesh):
    def step(x, dy, *state):
        x, dy = x[0], dy[0]
        weights = state[:3]
        at0, dyt, g0, u0, h1, a1, at1 = forward(x, dy, *weights)
        n = SPLIT[1]
        by1a, dga, dua = backward(1, 0, n, at1, dyt, dy, weights, a=a1)
        by1b, dgb, dub, r1a = backward(1, n, NB - n, at1, dyt, dy, weights, a=a1, before=by1a, after=(0, 2, 3, 3))
        by_h, by_ht, r1 = input_gradient((dga, dgb), (dua, dub), weights[0], weights[1], h1, dy, by1b, r1a, (1, 4, 6, 7))
        all1 = gather(r1)
        n = SPLIT[0]
        (by0a,) = backward(0, 0, n, at0, by_ht, by_h, weights, gu=(g0, u0))
        by0b, r0a = backward(0, n, NB - n, at0, by_ht, by_h, weights, gu=(g0, u0), before=by0a, after=(0, 2, 4, 4))
        r0, factor = reduce(by0b, r0a, r1)
        all0 = gather(r0)
        new = optimizer(1, factor, all1, state, None)
        new = optimizer(0, factor, all0, state, new)
        return tuple(new)

    return jax.shard_map(
        step,
        mesh=mesh,
        in_specs=(P(("rep", "dp"), None, None),) * 2 + (P(None, None, None),) * 9,
        out_specs=(P("rep", None, None),) * 9,
        check_vma=False,
    )
```

time: 661 us -> 399 us (0.60); the launches traced: 653 us -> 399 us
  Pallas kernels: 0 us -> 369 us
  matrix products: 259 us -> 0 us
  waiting for transfers between devices: 250 us -> 15.4 us
  other arithmetic: 116 us -> 0 us
  local copies, waits for them, and re-layouts: 12.3 us -> 0 us
    pallas_call x0 -> x9, Pallas kernels: none -> 369 us  [the longest x4 163 us: backward(): pl.pallas_call(functools.partial(block_body, last, hook), grid=(n,), in_s...]
    dot_general x15 -> x0, matrix products: 259 us -> none  [the longest x5 91.4 us: layer(): gate = jnp.dot(a, w['w_gate'], preferred_element_type=jnp.float32)]
    psum x1 -> x0, waiting for transfers between devices: 250 us -> none  [step(): summed[number] = [lax.psum(by_w[name], 'dp') for name in NAMES]]
    convert_element_type x2 -> x0, other arithmetic: 86.6 us -> none  [adamw(): return ((w - 0.02 * step).astype(jnp.bfloat16), m, v)]
    reduce_sum x4 -> x0, other arithmetic: 24.3 us -> none  [the longest x3 21.5 us: step(): jnp.sum(g * g)]
    all_gather x0 -> x2, waiting for transfers between devices: none -> 15.4 us  [gather(): return lax.all_gather(part.reshape(-1, *PANEL), 'dp')]
    unnamed x30 -> x0, local copies, waits for them, and re-layouts: 12.3 us -> none
  transfers between devices with their start and end apart: 1 -> 2, of which waited for: 1 -> 1; matrix products, arithmetic and copies ran while one was open for 0% -> 0% of each run, Pallas kernels for 0% -> 40%
where the time goes in v2:
time: 399 us
  Pallas kernels  369 us (92%)
  waiting for transfers between devices  15.4 us (4%)
  between operations  14.1 us (4%)
    pallas_call x4, Pallas kernels, backward(): pl.pallas_call(functools.partial(block_body, last, hook), grid=(n,), in_s...  163 us
    pallas_call x2, Pallas kernels, optimizer(): pl.pallas_call(optimizer_body, grid=(NB,), in_specs=[once((8, 128), lambd...  92.4 us
    pallas_call x1, Pallas kernels, forward(): pl.pallas_call(forward_body, grid=(T // TM,), in_specs=[row(D), row(D), w...  42.4 us
    pallas_call x1, Pallas kernels, reduce(): pl.pallas_call(reduce_body, in_specs=[ANY, vmem, vmem], out_specs=[vmem,...  36 us
    pallas_call x1, Pallas kernels, input_gradient(): pl.pallas_call(functools.partial(input_body, after), grid=(T // tm,), in_...  35.9 us
    all_gather x2, waiting for transfers between devices, gather(): return lax.all_gather(part.reshape(-1, *PANEL), 'dp')  15.4 us
  transfers between devices with their start and end apart: 2, of which 1 were waited for; matrix products, arithmetic and copies ran while one was open for 0% of the time, Pallas kernels for 40%

profile of v2, /device:TPU:0, one launch (start us, length us, event | category | flops | bytes accessed | tf_op | source)
XLA Modules:
  0.0 398.9 jit_solution(4092543102251088392)
XLA Ops:
  7.2 0.0 all-gather.5.cloned.1.call-start
  7.2 42.4 %fwd.1 = (bf16[896,2048]{1,0:T(8,128)(2,1)}, bf16[896,2048]{1,0:T(8,128)(2,1)}, f32[2048,2304]{1,0:T(8,128)}, f32[2048,2304]{1,0:T(8,128)}, bf16[2048,896]{1,0:T...) custom-call(bf16[2048,896]{1,0:T(8,128)(2,1)} %bitcast.10, bf16[2048,896]{1,0:T(8,128)(2,1)} %bitcast.11, ...), custom_call_target="tpu_custom_call" | custom-call | flops 25367150592 | bytes 75000000 | tf_op jit(solution)/shard_map/fwd/pallas_call | solution.py:74
  49.6 39.3 %bwd1a.1 = (bf16[2,3,5,8,112,128]{5,4,3,2,1,0:T(8,128)(2,1)}, bf16[2048,1280]{1,0:T(8,128)(2,1)}, bf16[2048,1280]{1,0:T(8,128)(2,1)}) custom-call(bf16[896,2048]{1,0:T(8,128)(2,1)} %get-tuple-element.40.refs_0_, bf16[896,2048]{1,0:T(8,128)(2,1)} %get-tuple-element.41.refs_1_, bf16[2048,896]{1,0:T(8,128)(2,1)} %bitcast.12, ...), custom_call_target="tpu_custom_call" | custom-call | flops 28185722880 | bytes 40000000 | tf_op jit(solution)/shard_map/bwd1a/pallas_call | solution.py:290
  88.9 44.7 %bwd1b.1 = (bf16[2,3,4,8,112,128]{5,4,3,2,1,0:T(8,128)(2,1)}, bf16[2048,1024]{1,0:T(8,128)(2,1)}, bf16[2048,1024]{1,0:T(8,128)(2,1)}, bf16[3,5,112,128]{3,2,1,0:T(8,128)(2,1)}) custom-call(bf16[896,2048]{1,0:T(8,128)(2,1)} %get-tuple-element.40.refs_0_, bf16[896,2048]{1,0:T(8,128)(2,1)} %get-tuple-element.41.refs_1_, bf16[2048,896]{1,0:T(8,128)(2,1)} %bitcast.13, ...), custom_call_target="tpu_custom_call" | custom-call | flops 22548578304 | bytes 32000000 | tf_op jit(solution)/shard_map/bwd1b/pallas_call | solution.py:290
  133.6 35.9 %bwd_in.1 = (bf16[2048,896]{1,0:T(8,128)(2,1)}, bf16[896,2048]{1,0:T(8,128)(2,1)}, bf16[3,9,112,128]{3,2,1,0:T(8,128)(2,1)}) custom-call(bf16[2048,1280]{1,0:T(8,128)(2,1)} %get-tuple-element.43.dga, bf16[2048,1024]{1,0:T(8,128)(2,1)} %get-tuple-element.45.dgb, bf16[2048,1280]{1,0:T(8,128)(2,1)} %get-tuple-element.46.dua, ...), custom_call_target="tpu_custom_call" | custom-call | flops 16911433728 | bytes 40000000 | tf_op jit(solution)/shard_map/bwd_in/pallas_call | solution.py:333
  169.5 0.0 all-gather.5.cloned.1.call-update
  169.5 0.0 all-gather.3.cloned.1.call-start
  169.6 26.3 %bwd0a.1.refs_6_ = bf16[2,3,4,8,112,128]{5,4,3,2,1,0:T(8,128)(2,1)} custom-call(bf16[896,2048]{1,0:T(8,128)(2,1)} %get-tuple-element.39.refs_0_, bf16[896,2048]{1,0:T(8,128)(2,1)} %get-tuple-element.51.refs_1_, bf16[2048,896]{1,0:T(8,128)(2,1)} %get-tuple-element.52.refs_2_, f32[2048,2304]{1,0:T(8,128)} %get-tuple-element.53.refs_3_, ...), custom_call_target="tpu_custom_call" | custom-call | flops 15032385536 | bytes 32000000 | tf_op jit(solution)/shard_map/bwd0a/pallas_call | solution.py:290
  195.9 52.2 %bwd0b.1 = (bf16[2,3,5,8,112,128]{5,4,3,2,1,0:T(8,128)(2,1)}, bf16[3,4,112,128]{3,2,1,0:T(8,128)(2,1)}) custom-call(bf16[896,2048]{1,0:T(8,128)(2,1)} %get-tuple-element.39.refs_0_, bf16[896,2048]{1,0:T(8,128)(2,1)} %get-tuple-element.51.refs_1_, bf16[2048,896]{1,0:T(8,128)(2,1)} %get-tuple-element.52.refs_2_, f32[2048,2304]{1,0:T(8,128)} %get-tuple-element.53.refs_3_, ...), custom_call_target="tpu_custom_call" | custom-call | flops 18790481920 | bytes 40000000 | tf_op jit(solution)/shard_map/bwd0b/pallas_call | solution.py:290
  248.2 36.0 %reduce0.1 = (bf16[3,9,112,128]{3,2,1,0:T(8,128)(2,1)}, f32[8,128]{1,0:T(8,128)}) custom-call(bf16[2,3,5,8,112,128]{5,4,3,2,1,0:T(8,128)(2,1)} %get-tuple-element.55.g, bf16[3,4,112,128]{3,2,1,0:T(8,128)(2,1)} %get-tuple-element.56.r_before, bf16[3,9,112,128]{3,2,1,0:T(8,128)(2,1)} %get-tuple-element.57.r1), custom_call_target="tpu_custom_call" | custom-call | flops 20000000000 | bytes 20000000 | tf_op jit(solution)/shard_map/reduce0/pallas_call | solution.py:388
  284.2 0.0 all-gather.3.cloned.1.call-update
  284.2 0.0 all-gather.5.cloned.1.call-done
  284.3 46.1 %adamw1.1 = (bf16[2,896,2304]{2,1,0:T(8,128)(2,1)}, bf16[2,896,2304]{2,1,0:T(8,128)(2,1)}, bf16[2,2304,896]{2,1,0:T(8,128)(2,1)}, f32[2,896,2304]{2,1,0:T(8,128)...) custom-call(f32[8,128]{1,0:T(8,128)} %get-tuple-element.58.factor, ...), custom_call_target="tpu_custom_call" | custom-call | flops 15000000512 | bytes 137000000 | tf_op jit(solution)/shard_map/adamw1/pallas_call | solution.py:433
  330.4 15.4 %all-gather.3.cloned.1.call-done = bf16[16,27,112,128]{3,2,1,0:T(8,128)(2,1)} async-done(((bf16[1,27,112,128]{3,2,1,0:T(8,128)(2,1)}), bf16[16,27,112,128]{3,2,1,0:T(8,128)(2,1)}) %all-gather.3.cloned.1.call-update) | async-done | bytes 12386320 | tf_op jit(solution)/shard_map/all_gather | solution.py:447
  345.7 46.3 %adamw0.1 = (bf16[2,896,2304]{2,1,0:T(8,128)(2,1)}, bf16[2,896,2304]{2,1,0:T(8,128)(2,1)}, bf16[2,2304,896]{2,1,0:T(8,128)(2,1)}, f32[2,896,2304]{2,1,0:T(8,128)...) custom-call(f32[8,128]{1,0:T(8,128)} %get-tuple-element.58.factor, ...), custom_call_target="tpu_custom_call", output_to_operand_aliasing={{0}: (11, {}), {1}: (12, {}), {2}: (13, {}), {3}: (14, {}),... | custom-call | flops 15000000512 | bytes 137000000 | tf_op jit(solution)/shard_map/adamw0/pallas_call | solution.py:433
Async XLA Ops:
  7.2 277.1 %all-gather.5.cloned.1.call-start = ((), (), s32[]{:S(2)}) async-start(), calls=%async_computation.1 | async-start | bytes 13160448 | tf_op jit(solution)/shard_map/all_gather | solution.py:447
  169.5 176.2 %all-gather.3.cloned.1.call-start = ((), (), s32[]{:S(2)}) async-start(), calls=%async_computation | async-start | bytes 13160448 | tf_op jit(solution)/shard_map/all_gather | solution.py:447
Sparse Core Ops, SparseCore 0:
  169.6 77.6 all-gather.4
  284.4 61.3 all-gather.2

commit v3 on v2

--- a/solution.py
+++ b/solution.py
@@ -12,7 +12,7 @@
 LAYERS, T, D, FF = 2, 2048, 896, 2304
 FB = 256
 NB = FF // FB
-SPLIT = {1: 5, 0: 4}
+SPLIT = 4
 TM = 512
 RG = D // 8
 PANEL = (RG, 128)
@@ -221,18 +221,11 @@
     (out,) = take(1)
     dgo, duo = take(2) if last else (None, None)
     r = take(1)[0] if hook else None
-    ps, dgs, dus, atv, dytv, sem = take(6)
+    ps, dgs, dus = take(3)
     b = pl.program_id(0)
     if hook:
         before, behind = Reduction(hook[0], g_before, refs).hooks(b, hook[1], r)
         before()
-    loads = pltpu.make_async_copy(at, atv, sem.at[0]), pltpu.make_async_copy(dyt, dytv, sem.at[1])
-
-    @pl.when(b == 0)
-    def _():
-        for load in loads:
-            load.start()
-
     for i in range(T // TM):
         rows = slice(i * TM, (i + 1) * TM)
         dp = dot(dy[rows, :], wd[0], 1, 1).astype(BF16).astype(F32)
@@ -252,12 +245,7 @@
             dgo[rows, :] = dg
             duo[rows, :] = du
 
-    @pl.when(b == 0)
-    def _():
-        for load in loads:
-            load.wait()
-
-    for m, (lhs, rhs) in enumerate(((atv, dgs), (atv, dus), (dytv, ps))):
+    for m, (lhs, rhs) in enumerate(((at, dgs), (at, dus), (dyt, ps))):
         full = dot(lhs[...], rhs[...], 1, 0)
         for k in range(8):
             for c in range(2):
@@ -278,7 +266,7 @@
     if last:
         out_specs += [pl.BlockSpec((T, FB), lambda b: (0, b))] * 2
         out_shape += [jax.ShapeDtypeStruct((T, n * FB), BF16)] * 2
-    scratch = [pltpu.VMEM((T, FB), BF16)] * 3 + [pltpu.VMEM((D, T), BF16)] * 2 + [pltpu.SemaphoreType.DMA((2,))]
+    scratch = [pltpu.VMEM((T, FB), BF16)] * 3
     hook, more = None, {}
     if before is not None:
         nb = before.shape[2]
@@ -290,7 +278,7 @@
     return pl.pallas_call(
         functools.partial(block_body, last, hook),
         grid=(n,),
-        in_specs=[ANY, ANY, full((T, D)), *in_specs],
+        in_specs=[full((D, T)), full((D, T)), full((T, D)), *in_specs],
         out_specs=out_specs,
         out_shape=out_shape,
         scratch_shapes=scratch,
@@ -343,17 +331,15 @@
     )(*dgs, *dus, wg, wu, h, dy, g_before, r_before)
 
 
-def reduce_body(g, r_before, r1, r0, factor, part, nb, norm_sem, *scratch):
-    blocks = g.shape[2]
-    reduction = Reduction(blocks, g, scratch)
+def reduce_body(g, r1, r0, factor, part, nb, norm_sem, *scratch):
+    reduction = Reduction(NB, g, scratch)
     me = reduction.me
     reduction.barrier(True)
     reduction.start()
-    r0[:, : NB - blocks] = r_before[...]
     reduction.stage1()
     reduction.stage2()
     reduction.stage3()
-    reduction.finish(r0, NB - blocks)
+    reduction.finish(r0)
     part[...] = jnp.zeros_like(part)
 
     def squares(b, carry):
@@ -383,18 +369,18 @@
     factor[...] = jnp.broadcast_to(jnp.minimum(1.0, 0.5 * lax.rsqrt(total / (LAYERS * 3 * D * FF) + 1e-30)), factor.shape)
 
 
-def reduce(g, r_before, r1):
+def reduce(g, r1):
     vmem = pl.BlockSpec(memory_space=pltpu.VMEM)
     return pl.pallas_call(
         reduce_body,
-        in_specs=[ANY, vmem, vmem],
+        in_specs=[ANY, vmem],
         out_specs=[vmem, vmem],
         out_shape=[jax.ShapeDtypeStruct((3, NB, *PANEL), BF16), jax.ShapeDtypeStruct((8, 128), F32)],
-        scratch_shapes=[pltpu.VMEM((8, 128), F32), pltpu.VMEM((16, 8, 128), F32), pltpu.SemaphoreType.DMA((2, 16)), *Reduction.scratch(g.shape[2])],
+        scratch_shapes=[pltpu.VMEM((8, 128), F32), pltpu.VMEM((16, 8, 128), F32), pltpu.SemaphoreType.DMA((2, 16)), *Reduction.scratch(NB)],
         compiler_params=pltpu.CompilerParams(collective_id=0, has_side_effects=True, vmem_limit_bytes=VMEM),
         cost_estimate=cost(20_000_000_000, 20_000_000),
         name="reduce0",
-    )(g, r_before, r1)
+    )(g, r1)
 
 
 def adamw(w, m, v, g):
@@ -452,15 +438,13 @@
         x, dy = x[0], dy[0]
         weights = state[:3]
         at0, dyt, g0, u0, h1, a1, at1 = forward(x, dy, *weights)
-        n = SPLIT[1]
+        n = SPLIT
         by1a, dga, dua = backward(1, 0, n, at1, dyt, dy, weights, a=a1)
-        by1b, dgb, dub, r1a = backward(1, n, NB - n, at1, dyt, dy, weights, a=a1, before=by1a, after=(0, 2, 3, 3))
-        by_h, by_ht, r1 = input_gradient((dga, dgb), (dua, dub), weights[0], weights[1], h1, dy, by1b, r1a, (1, 4, 6, 7))
+        by1b, dgb, dub, r1a = backward(1, n, NB - n, at1, dyt, dy, weights, a=a1, before=by1a, after=(0, 2, 3, 4))
+        by_h, by_ht, r1 = input_gradient((dga, dgb), (dua, dub), weights[0], weights[1], h1, dy, by1b, r1a, (1, 5, 7, 7))
         all1 = gather(r1)
-        n = SPLIT[0]
-        (by0a,) = backward(0, 0, n, at0, by_ht, by_h, weights, gu=(g0, u0))
-        by0b, r0a = backward(0, n, NB - n, at0, by_ht, by_h, weights, gu=(g0, u0), before=by0a, after=(0, 2, 4, 4))
-        r0, factor = reduce(by0b, r0a, r1)
+        (by0,) = backward(0, 0, NB, at0, by_ht, by_h, weights, gu=(g0, u0))
+        r0, factor = reduce(by0, r1)
         all0 = gather(r0)
         new = optimizer(1, factor, all1, state, None)
         new = optimizer(0, factor, all0, state, new)

time: 399 us -> 391 us (0.980)
  Pallas kernels: 369 us -> 361 us
    pallas_call x4 -> x3, Pallas kernels: 163 us -> 127 us  [backward(): pl.pallas_call(functools.partial(block_body, last, hook), grid=(n,), in_s...]
    pallas_call x1, Pallas kernels: 36 us -> 59.3 us  [reduce(): pl.pallas_call(reduce_body, in_specs=[ANY, vmem], out_specs=[vmem, vmem],...]
    pallas_call x1, Pallas kernels: 35.9 us -> 40.1 us  [input_gradient(): pl.pallas_call(functools.partial(input_body, after), grid=(T // tm,), in_...]
  transfers between devices with their start and end apart: 2 -> 2, of which waited for: 1 -> 1; matrix products, arithmetic and copies ran while one was open for 0% -> 0% of each run, Pallas kernels for 40% -> 39%
where the time goes in v3:
time: 391 us; the launch traced here: 390 us
  Pallas kernels  361 us (92%)
  waiting for transfers between devices  14.9 us (4%)
  between operations  14.1 us (4%)
    pallas_call x3, Pallas kernels, backward(): pl.pallas_call(functools.partial(block_body, last, hook), grid=(n,), in_s...  127 us
    pallas_call x2, Pallas kernels, optimizer(): pl.pallas_call(optimizer_body, grid=(NB,), in_specs=[once((8, 128), lambd...  92.2 us
    pallas_call x1, Pallas kernels, reduce(): pl.pallas_call(reduce_body, in_specs=[ANY, vmem], out_specs=[vmem, vmem],...  59.3 us
    pallas_call x1, Pallas kernels, forward(): pl.pallas_call(forward_body, grid=(T // TM,), in_specs=[row(D), row(D), w...  42.3 us
    pallas_call x1, Pallas kernels, input_gradient(): pl.pallas_call(functools.partial(input_body, after), grid=(T // tm,), in_...  40.1 us
    all_gather x2, waiting for transfers between devices, gather(): return lax.all_gather(part.reshape(-1, *PANEL), 'dp')  14.9 us
  transfers between devices with their start and end apart: 2, of which 1 were waited for; matrix products, arithmetic and copies ran while one was open for 0% of the time, Pallas kernels for 39%

profile of v3, /device:TPU:0, one launch (start us, length us, event | category | flops | bytes accessed | tf_op | source)
XLA Modules:
  0.0 390.4 jit_solution(2334418821267041761)
XLA Ops:
  7.2 0.0 all-gather.5.cloned.1.call-start
  7.2 42.3 %fwd.1 = (bf16[896,2048]{1,0:T(8,128)(2,1)}, bf16[896,2048]{1,0:T(8,128)(2,1)}, f32[2048,2304]{1,0:T(8,128)}, f32[2048,2304]{1,0:T(8,128)}, bf16[2048,896]{1,0:T...) custom-call(bf16[2048,896]{1,0:T(8,128)(2,1)} %bitcast.10, bf16[2048,896]{1,0:T(8,128)(2,1)} %bitcast.11, ...), custom_call_target="tpu_custom_call" | custom-call | flops 25367150592 | bytes 75000000 | tf_op jit(solution)/shard_map/fwd/pallas_call | solution.py:74
  49.6 34.0 %bwd1a.1 = (bf16[2,3,4,8,112,128]{5,4,3,2,1,0:T(8,128)(2,1)}, bf16[2048,1024]{1,0:T(8,128)(2,1)}, bf16[2048,1024]{1,0:T(8,128)(2,1)}) custom-call(bf16[896,2048]{1,0:T(8,128)(2,1)} %get-tuple-element.38.refs_0_, bf16[896,2048]{1,0:T(8,128)(2,1)} %get-tuple-element.39.refs_1_, bf16[2048,896]{1,0:T(8,128)(2,1)} %bitcast.12, ...), custom_call_target="tpu_custom_call" | custom-call | flops 22548578304 | bytes 32000000 | tf_op jit(solution)/shard_map/bwd1a/pallas_call | solution.py:278
  83.6 46.9 %bwd1b.1 = (bf16[2,3,5,8,112,128]{5,4,3,2,1,0:T(8,128)(2,1)}, bf16[2048,1280]{1,0:T(8,128)(2,1)}, bf16[2048,1280]{1,0:T(8,128)(2,1)}, bf16[3,4,112,128]{3,2,1,0:T(8,128)(2,1)}) custom-call(bf16[896,2048]{1,0:T(8,128)(2,1)} %get-tuple-element.38.refs_0_, bf16[896,2048]{1,0:T(8,128)(2,1)} %get-tuple-element.39.refs_1_, bf16[2048,896]{1,0:T(8,128)(2,1)} %bitcast.13, ...), custom_call_target="tpu_custom_call" | custom-call | flops 28185722880 | bytes 40000000 | tf_op jit(solution)/shard_map/bwd1b/pallas_call | solution.py:278
  130.5 40.1 %bwd_in.1 = (bf16[2048,896]{1,0:T(8,128)(2,1)}, bf16[896,2048]{1,0:T(8,128)(2,1)}, bf16[3,9,112,128]{3,2,1,0:T(8,128)(2,1)}) custom-call(bf16[2048,1024]{1,0:T(8,128)(2,1)} %get-tuple-element.41.dga, bf16[2048,1280]{1,0:T(8,128)(2,1)} %get-tuple-element.43.dgb, bf16[2048,1024]{1,0:T(8,128)(2,1)} %get-tuple-element.44.dua, ...), custom_call_target="tpu_custom_call" | custom-call | flops 16911433728 | bytes 40000000 | tf_op jit(solution)/shard_map/bwd_in/pallas_call | solution.py:321
  170.5 0.0 all-gather.5.cloned.1.call-update
  170.6 0.0 all-gather.3.cloned.1.call-start
  170.6 46.5 %bwd0a.1.g = bf16[2,3,9,8,112,128]{5,4,3,2,1,0:T(8,128)(2,1)} custom-call(bf16[896,2048]{1,0:T(8,128)(2,1)} %get-tuple-element.37.refs_0_, bf16[896,2048]{1,0:T(8,128)(2,1)} %get-tuple-element.49.refs_1_, bf16[2048,896]{1,0:T(8,128)(2,1)} %get-tuple-element.50.refs_2_, f32[2048,2304]{1,0:T(8,128)} %get-tuple-element.51.refs_3_, ...), custom_call_target="tpu_custom_call" | custom-call | flops 33822867456 | bytes 72000000 | tf_op jit(solution)/shard_map/bwd0a/pallas_call | solution.py:278
  217.1 59.3 %reduce0.1 = (bf16[3,9,112,128]{3,2,1,0:T(8,128)(2,1)}, f32[8,128]{1,0:T(8,128)}) custom-call(bf16[2,3,9,8,112,128]{5,4,3,2,1,0:T(8,128)(2,1)} %bwd0a.1.g, bf16[3,9,112,128]{3,2,1,0:T(8,128)(2,1)} %get-tuple-element.53.r1), custom_call_target="tpu_custom_call" | custom-call | flops 20000000000 | bytes 20000000 | tf_op jit(solution)/shard_map/reduce0/pallas_call | solution.py:374
  276.4 0.0 all-gather.3.cloned.1.call-update
  276.4 0.0 all-gather.5.cloned.1.call-done
  276.5 46.1 %adamw1.1 = (bf16[2,896,2304]{2,1,0:T(8,128)(2,1)}, bf16[2,896,2304]{2,1,0:T(8,128)(2,1)}, bf16[2,2304,896]{2,1,0:T(8,128)(2,1)}, f32[2,896,2304]{2,1,0:T(8,128)...) custom-call(f32[8,128]{1,0:T(8,128)} %get-tuple-element.54.factor, ...), custom_call_target="tpu_custom_call" | custom-call | flops 15000000512 | bytes 137000000 | tf_op jit(solution)/shard_map/adamw1/pallas_call | solution.py:419
  322.6 14.9 %all-gather.3.cloned.1.call-done = bf16[16,27,112,128]{3,2,1,0:T(8,128)(2,1)} async-done(((bf16[1,27,112,128]{3,2,1,0:T(8,128)(2,1)}), bf16[16,27,112,128]{3,2,1,0:T(8,128)(2,1)}) %all-gather.3.cloned.1.call-update) | async-done | bytes 12386320 | tf_op jit(solution)/shard_map/all_gather | solution.py:433
  337.4 46.1 %adamw0.1 = (bf16[2,896,2304]{2,1,0:T(8,128)(2,1)}, bf16[2,896,2304]{2,1,0:T(8,128)(2,1)}, bf16[2,2304,896]{2,1,0:T(8,128)(2,1)}, f32[2,896,2304]{2,1,0:T(8,128)...) custom-call(f32[8,128]{1,0:T(8,128)} %get-tuple-element.54.factor, ...), custom_call_target="tpu_custom_call", output_to_operand_aliasing={{0}: (11, {}), {1}: (12, {}), {2}: (13, {}), {3}: (14, {}),... | custom-call | flops 15000000512 | bytes 137000000 | tf_op jit(solution)/shard_map/adamw0/pallas_call | solution.py:419
Async XLA Ops:
  7.2 269.3 %all-gather.5.cloned.1.call-start = ((), (), s32[]{:S(2)}) async-start(), calls=%async_computation.1 | async-start | bytes 13160448 | tf_op jit(solution)/shard_map/all_gather | solution.py:433
  170.6 166.9 %all-gather.3.cloned.1.call-start = ((), (), s32[]{:S(2)}) async-start(), calls=%async_computation | async-start | bytes 13160448 | tf_op jit(solution)/shard_map/all_gather | solution.py:433
Sparse Core Ops, SparseCore 0:
  170.7 67.2 all-gather.4
  276.5 60.8 all-gather.2
